TPU v7x, 128 devices: a whole 4x4x4 slice. The times are simulated.
128 devices in a mesh: dp: 8 (over x_lo, y), tensor: 16 (over x_hi, z, core).
Axes of the slice: x: 4 (x_hi: 2, x_lo: 2; x = x_hi * 2 + x_lo), y: 4, z: 4, core: 2. Of those that a mesh axis runs over, the one named last changes fastest.
Arguments:
- activations: bfloat16 [12288, 8192], P('dp', 'tensor'), may hold values from -6 to 6
- deltas: bfloat16 [12288, 28672], P('dp', 'tensor'), may hold values from -6 to 6
- query_in: bfloat16 [8192, 1024], P('tensor', 'dp'), may hold values from -0.0625 to 0.0625
- query_out: bfloat16 [28672, 1024], P('tensor', 'dp'), may hold values from -0.03125 to 0.03125
- doc_ids: int32 [12288], P('dp'), may hold values from 0 to 63, never falling along the last dimension, each value on 1 to 384 neighbouring positions
Outputs:
- scores: float32 [12288, 32], P('dp')
- doc_scores: float32 [64, 32], replicated
Inputs may be any that keep to these rules, and one draw needn't show every extreme that they name: doc_ids never falls along the tokens; every document owns 1 to 384 tokens, and one owns exactly 384.
All inputs are finite; a program needn't handle non-finite values.
Results may differ from a plain program's by a relative error of at most 0.0003.
Values may be sent and summed in bfloat16 or wider, within the bound.
A program may use at most 128 MiB of HBM per device.

v0:
```python
import jax
import jax.numpy as jnp
from jax import lax
from jax.sharding import PartitionSpec as P

RANK = 32
DOC_DEV = 8


def side_by_side(arrays, axis, dim, along):
    both = jnp.concatenate(arrays, axis=along)
    filled, at, done = (lax.all_gather(both, axis, axis=dim, tiled=True), 0, [])
    for a in arrays:
        done.append(lax.slice_in_dim(filled, at, at + a.shape[along], axis=along))
        at += a.shape[along]
    return tuple(done)


def sent_together(arrays, axis, dim, along):
    widths = [a.shape[along] for a in arrays]
    both = jnp.concatenate(arrays, axis=along)
    filled = lax.psum_scatter(both, axis, scatter_dimension=dim, tiled=True)
    return tuple(jnp.split(filled, [sum(widths[:k]) for k in range(1, len(widths))], axis=along))


def copy_for_each(array, axis):
    copies = jnp.broadcast_to(array, (lax.axis_size(axis), *array.shape))
    return lax.all_to_all(copies, axis, split_axis=0, concat_axis=0, tiled=True)


def joined_along(blocks, dim):
    blocks = jnp.moveaxis(blocks, 0, dim)
    shape = blocks.shape
    return blocks.reshape(*shape[:dim], shape[dim] * shape[dim + 1], *shape[dim + 2 :])


def gather_directly(array, axis, dim):
    blocks = copy_for_each(array, axis)
    return joined_along(blocks, dim)


def taken_together(array, axis):
    return copy_for_each(array, axis).sum(axis=0)


def packed_total(arrays, axis):
    ends = [0]
    for a in arrays:
        ends.append(ends[-1] + a.size)
    running = taken_together(jnp.concatenate([a.ravel() for a in arrays]), axis)
    return tuple((running[b:e].reshape(a.shape) for a, b, e in zip(arrays, ends, ends[1:])))


def score_rows(left, right):
    queries = left.shape[1] // RANK
    products = (left * right).reshape(left.shape[0], queries, RANK)
    return jnp.sum(products, axis=2) * jnp.float32(RANK ** (-0.5))


def body(activations, deltas, query_in, query_out, doc_ids):
    rows = activations.shape[0]
    full_in, full_out = side_by_side((query_in, query_out), "dp", 1, 0)
    proj_in = jnp.dot(activations, full_in, preferred_element_type=jnp.float32)
    proj_out = jnp.dot(deltas, full_out, preferred_element_type=jnp.float32)
    share_in, share_out = sent_together((proj_in, proj_out), "tensor", 0, 1)
    scores = gather_directly(score_rows(share_in, share_out), "tensor", 0)
    queries = scores.shape[1]
    first = doc_ids[0]
    local = doc_ids - first
    slots = lax.iota(jnp.int32, rows)
    onehot = (slots[:, None] == local[None, :]).astype(jnp.float32)
    sums = jnp.dot(
        onehot, scores, precision=lax.Precision.HIGHEST, preferred_element_type=jnp.float32
    )
    counts = jnp.sum(onehot, axis=1)
    total_docs = DOC_DEV * lax.axis_size("dp")
    placed = lax.dynamic_update_slice_in_dim(
        jnp.zeros((total_docs + rows, queries), jnp.float32), sums, first, 0
    )[:total_docs]
    placed_counts = lax.dynamic_update_slice_in_dim(
        jnp.zeros((total_docs + rows,), jnp.float32), counts, first, 0
    )[:total_docs]
    doc_sums, doc_counts = packed_total((placed, placed_counts), "dp")
    doc_scores = doc_sums / jnp.maximum(doc_counts, 1.0)[:, None]
    return (scores, doc_scores)


def solution(mesh):
    return jax.shard_map(
        body,
        mesh=mesh,
        in_specs=(
            P("dp", "tensor"),
            P("dp", "tensor"),
            P("tensor", "dp"),
            P("tensor", "dp"),
            P("dp"),
        ),
        out_specs=(P("dp", None), P()),
        check_vma=False,
    )
```

profile of v0, /device:TPU:1, one launch (start us, length us, event | category | flops | bytes accessed | tf_op | source)
XLA Modules:
  0.0 281.0 jit_solution(15343516209380686068)
XLA Ops:
  7.2 0.0 copy-start
  7.2 0.0 all-gather.2.cloned.1.call-start
  7.2 2.0 pad_maximum_fusion.1
  9.2 0.0 all-gather.2.cloned.1.call-update
  9.3 0.0 reduce-scatter.4.cloned.1.call-start
  9.3 63.1 %all-gather.2.cloned.1.call-done = bf16[2304,1024]{1,0:T(8,128)(2,1)} async-done(((bf16[2304,128]{1,0:T(8,128)(2,1)}), bf16[2304,1024]{1,0:T(8,128)(2,1)}) %all-gather.2.cloned.1.call-update) | async-done | bytes 4718608 | tf_op jit(solution)/shard_map/all_gather | solution.py:12
  72.4 10.9 %convolution_bitcast_fusion = f32[1536,1024]{0,1:T(8,128)} fusion(bf16[1536,1792]{1,0:T(8,128)(2,1)} %param.6, bf16[2304,1024]{1,0:T(8,128)(2,1)} %all-gather.2.cloned.1.call-done), kind=kOutput, calls=%fused_computation.5 | convolution fusion | flops 5637144576 | bytes 15466496 | tf_op jit(solution)/shard_map/dot_general | solution.py:64
  83.3 0.0 copy-done
  83.3 5.7 %convolution_bitcast_fusion.1 = f32[1536,1024]{0,1:T(8,128)} fusion(bf16[1536,512]{1,0:T(8,128)(2,1)S(1)} %copy-done, bf16[2304,1024]{1,0:T(8,128)(2,1)} %all-gather.2.cloned.1.call-done), kind=kOutput, calls=%fused_computation.6 | convolution fusion | flops 1610612736 | bytes 8912896 | tf_op jit(solution)/shard_map/dot_general | solution.py:63
  89.0 10.4 %pad_maximum_fusion = f32[1536,2048]{0,1:T(8,128)} fusion(f32[1536,1024]{0,1:T(8,128)} %convolution_bitcast_fusion, f32[1536,1024]{0,1:T(8,128)} %convolution_bitcast_fusion.1), kind=kLoop, calls=%fused_computation | loop fusion | flops 3145728 | bytes 25165824 | tf_op jit(solution)/shard_map/concatenate | solution.py:21
  99.4 12.7 %copy.22 = f32[1536,2048]{1,0:T(8,128)} copy(f32[1536,2048]{0,1:T(8,128)} %pad_maximum_fusion) | data formatting | bytes 25165824
  112.2 0.0 copy-start.2
  112.2 0.0 reduce-scatter.4.cloned.1.call-update
  112.2 0.7 copy-done.2
  112.9 0.5 slice.31
  115.3 0.6 broadcast_subtract_fusion
  116.0 123.5 %reduce-scatter.4.cloned.1.call-done = f32[96,2048]{1,0:T(8,128)} async-done(((f32[1536,2048]{1,0:T(8,128)}), f32[96,2048]{1,0:T(8,128)}) %reduce-scatter.4.cloned.1.call-update) | async-done | bytes 786448
  239.5 1.2 fusion.4
  240.6 0.2 copy.25
  240.8 0.2 copy.26
  241.0 0.1 bitcast_reduce_fusion
  241.2 0.7 broadcast_in_dim.15
  241.9 5.0 %all-to-all-start = ((f32[16,96,32]{1,2,0:T(8,128)}), f32[16,96,32]{1,2,0:T(8,128)S(1)}, u32[]{:S(2)}, u32[]{:S(2)}) async-start(f32[16,96,32]{1,2,0:T(8,128)} %broadcast_in_dim.15), calls=%async_computation | async-start | bytes 524288 | tf_op jit(solution)/shard_map/all_to_all | solution.py:28
  246.9 1.0 convert_reduce_fusion
  247.9 0.3 dynamic_update_slice.7
  248.2 7.4 %all-to-all-done = f32[16,96,32]{1,2,0:T(8,128)S(1)} async-done(((f32[16,96,32]{1,2,0:T(8,128)}), f32[16,96,32]{1,2,0:T(8,128)S(1)}, u32[]{:S(2)}, u32[]{:S(2)}) %all-to-all-start) | async-done | bytes 196640 | tf_op jit(solution)/shard_map/all_to_all | solution.py:28
  255.6 0.2 copy.17
  255.8 0.1 reshape.31
  255.9 0.0 copy-start.1
  255.9 4.2 %fusion = f32[1536,32]{1,0:T(8,128)S(1)} fusion(f32[1536,32]{0,1:T(8,128)S(1)} %reshape.31, s32[1536]{0:T(1024)S(1)} %broadcast_subtract_fusion), kind=kOutput, calls=%fused_computation.3 | convolution fusion | flops 908328960 | bytes 399360 | tf_op jit(solution)/shard_map/dot_general | solution.py:72
  260.1 0.1 broadcast_in_dim.16
  260.2 3.1 %dynamic_update_slice.6 = f32[1600,32]{1,0:T(8,128)S(1)} dynamic-update-slice(f32[1600,32]{1,0:T(8,128)S(1)} %broadcast_in_dim.16, f32[1536,32]{1,0:T(8,128)S(1)} %fusion, s32[]{:T(128)S(6)} %select_n.4, s32[]{:T(128)} %constant.0.clone.1) | dynamic-update-slice | bytes 393220 | tf_op jit(solution)/shard_map/dynamic_update_slice | solution.py:77
  263.3 0.1 reshape.32
  263.4 9.8 %all_to_all.11 = f32[8,1,2112]{2,1,0:T(1,128)S(1)} all-to-all(f32[8,1,2112]{2,1,0:T(1,128)S(1)} %broadcast_in_dim.18), channel_id=1, replica_groups=mesh['dp'=8,'tensor'=16] {'dp'}, dimensions={0} | all-to-all | bytes 135168 | tf_op jit(solution)/shard_map/all_to_all | solution.py:28
  273.2 0.1 reduce_sum.29
  273.3 0.1 reshape.33
  273.4 0.1 broadcast_divide_fusion
  273.5 0.7 copy.20
  274.2 0.0 copy-done.1
  (8 shorter events, 0.1 us)
Async XLA Ops:
  7.2 76.2 %copy-start = (bf16[1536,512]{1,0:T(8,128)(2,1)S(1)}, bf16[1536,512]{1,0:T(8,128)(2,1)}, u32[]{:S(2)}) copy-start(bf16[1536,512]{1,0:T(8,128)(2,1)} %param.5) | copy-start | bytes 4718596
  7.2 65.3 %all-gather.2.cloned.1.call-start = ((), (), s32[]{:S(2)}) async-start(), calls=%async_computation.3 | async-start | bytes 5308416 | tf_op jit(solution)/shard_map/all_gather | solution.py:12
  9.3 230.2 %reduce-scatter.4.cloned.1.call-start = ((), (), s32[]{:S(2)}) async-start(), calls=%async_computation.4 | async-start | bytes 13369344
  112.2 0.7 copy-start.2
  241.9 13.7 %all-to-all-start = ((f32[16,96,32]{1,2,0:T(8,128)}), f32[16,96,32]{1,2,0:T(8,128)S(1)}, u32[]{:S(2)}, u32[]{:S(2)}) async-start(f32[16,96,32]{1,2,0:T(8,128)} %broadcast_in_dim.15), calls=%async_computation | async-start | bytes 524288 | tf_op jit(solution)/shard_map/all_to_all | solution.py:28
  255.9 18.3 %copy-start.1 = (f32[1536,32]{0,1:T(8,128)}, f32[1536,32]{0,1:T(8,128)S(1)}, u32[]{:S(2)}) copy-start(f32[1536,32]{0,1:T(8,128)S(1)} %reshape.31) | copy-start | bytes 589828
Sparse Core Ops, SparseCore 0:
  9.6 62.8 all-gather.1
  112.3 127.1 reduce-scatter.3
where the time goes:
time: 283 us; the launch traced here: 281 us
  waiting for transfers between devices  194 us (69%)
  local copies, waits for them, and re-layouts  20.8 us (7%)
  matrix products  20.8 us (7%)
  between operations  16.1 us (6%)
  other arithmetic  14.4 us (5%)
  blocking collectives  9.83 us (3%)
  starting transfers between devices  5.07 us (2%)
    unnamed x3, waiting for transfers between devices  124 us
    all_gather x1, waiting for transfers between devices, side_by_side(): filled, at, done = (lax.all_gather(both, axis, axis=dim, tiled=True), 0, [])  63.1 us
    unnamed x10, local copies, waits for them, and re-layouts  14.5 us
    dot_general x1, matrix products, body(): proj_out = jnp.dot(deltas, full_out, preferred_element_type=jnp.float32)  10.9 us
    concatenate x1, other arithmetic, sent_together(): both = jnp.concatenate(arrays, axis=along)  10.4 us
    all_to_all x1, blocking collectives, copy_for_each(): return lax.all_to_all(copies, axis, split_axis=0, concat_axis=0, tiled=True)  9.83 us
    all_to_all x1, waiting for transfers between devices, copy_for_each(): return lax.all_to_all(copies, axis, split_axis=0, concat_axis=0, tiled=True)  7.38 us
    dot_general x1, matrix products, body(): proj_in = jnp.dot(activations, full_in, preferred_element_type=jnp.float32)  5.67 us
  transfers between devices with their start and end apart: 3, of which 3 were waited for; matrix products, arithmetic and copies ran while one was open for 1% of the time, Pallas kernels for 0%

commit v1 on v0

v1 whole, which is shorter than its diff:
```python
import jax
import jax.numpy as jnp
from jax import lax
from jax.experimental import pallas as pl
from jax.experimental.pallas import tpu as pltpu
from jax.sharding import PartitionSpec as P

RANK = 32
MESH = pl.DeviceIdType.MESH
F32 = jnp.float32
HIGHEST = lax.Precision.HIGHEST

ROWS = 1536
HALF = ROWS // 2
ZCH = HALF // 4
CH = ZCH // 2
KIN = 512
KOUT = 1792
K = KIN + KOUT
KH = K // 2
NB = 8
TM = 256
D2D, HA, HB, RMA, RMB, RPA, RPB, XH = range(8)


def nt(a, b):
    return lax.dot_general(
        a, b, (((1,), (1,)), ((), ())), precision=HIGHEST, preferred_element_type=F32
    )


def kernel(
    act, dl, qi, qo, ids, scores_out, docs_out,
    a_in, a_out, q, p, dbuf, h, rm, rp, xb, acc, msg, g, dpb,
    lsem, qs, qr, rs, rr, gs, gr, ds_, dr,
):
    dp = lax.axis_index("dp")
    t = lax.axis_index("tensor")
    xl, y = dp // 4, dp % 4
    hx, z, c = t // 8, (t // 2) % 4, t % 2

    x_lo = {"dp": (dp + 4) % 8, "tensor": t}
    y_up = {"dp": xl * 4 + (y + 1) % 4, "tensor": t}
    y_dn = {"dp": xl * 4 + (y + 3) % 4, "tensor": t}
    x_hi = {"dp": dp, "tensor": (t + 8) % 16}
    z_up = {"dp": dp, "tensor": hx * 8 + ((z + 1) % 4) * 2 + c}
    z_dn = {"dp": dp, "tensor": hx * 8 + ((z + 3) % 4) * 2 + c}
    mate = {"dp": dp, "tensor": hx * 8 + z * 2 + 1 - c}

    loads = [
        pltpu.make_async_copy(qi, q.at[0, pl.ds(0, KIN)], lsem.at[0]),
        pltpu.make_async_copy(qo, q.at[0, pl.ds(KIN, KOUT)], lsem.at[1]),
        pltpu.make_async_copy(act, a_in, lsem.at[2]),
        pltpu.make_async_copy(dl, a_out, lsem.at[3]),
    ]
    for cp in loads:
        cp.start()

    barrier = pltpu.get_barrier_semaphore()
    for k in range(1, 16):
        pl.semaphore_signal(
            barrier, inc=1, device_id={"dp": dp, "tensor": (t + k) % 16}, device_id_type=MESH
        )
    for k in range(1, 8):
        pl.semaphore_signal(
            barrier, inc=1, device_id={"dp": (dp + k) % 8, "tensor": t}, device_id_type=MESH
        )
    pl.semaphore_wait(barrier, 22)

    sent = []

    def send(src, dst, ss, rsem, to):
        cp = pltpu.make_async_remote_copy(
            src_ref=src, dst_ref=dst, send_sem=ss, recv_sem=rsem,
            device_id=to, device_id_type=MESH,
        )
        cp.start()
        sent.append(cp)
        return cp

    lo, hi, full = pl.ds(0, KH), pl.ds(KH, KH), pl.ds(0, K)

    def qsend(n, src, dst, rows, to):
        return send(q.at[src, rows], q.at[dst, rows], qs.at[n], qr.at[n], to)

    loads[0].wait()
    loads[1].wait()
    q1 = qsend(0, 0, 1, full, x_lo)
    q3 = qsend(1, 0, 3, full, y_up)
    q2 = qsend(2, 0, 2, full, y_dn)
    loads[2].wait()
    loads[3].wait()

    moves = {}

    def rsend(b, role, src, dst, to):
        moves[b, role] = send(src, dst, rs.at[role, b], rr.at[role, b], to)

    own, other = c * HALF, (1 - c) * HALF

    def zrows(dz, part=0, n=CH):
        at = own + ((z + dz) % 4) * ZCH + part * CH
        return pl.ds(pl.multiple_of(at, CH), n)

    def mm(b):
        for base in (other, own):

            def tile(i, carry, base=base):
                rows = pl.ds(pl.multiple_of(base + i * TM, TM), TM)
                p[b, rows, pl.ds(0, 128)] = jnp.dot(
                    a_in[rows, :], q[b, pl.ds(0, KIN), :], preferred_element_type=F32
                )
                p[b, rows, pl.ds(128, 128)] = jnp.dot(
                    a_out[rows, :], q[b, pl.ds(KIN, KOUT), :], preferred_element_type=F32
                )
                return carry

            lax.fori_loop(0, HALF // TM, tile, 0)
            if base is other:
                rsend(b, D2D, p.at[b, pl.ds(pl.multiple_of(other, HALF), HALF)], dbuf.at[b], mate)

    def step1(b):
        moves[b, D2D].wait_recv()
        rows = pl.ds(pl.multiple_of(own, HALF), HALF)
        p[b, rows, :] += dbuf[b]
        rsend(b, HA, p.at[b, zrows(2, 0)], h.at[b, 0], z_up)
        rsend(b, HB, p.at[b, zrows(2, 1)], h.at[b, 1], z_dn)
        rsend(b, RMB, p.at[b, zrows(1, 1)], rm.at[b, 1], z_up)
        rsend(b, RPA, p.at[b, zrows(3, 0)], rp.at[b, 0], z_dn)

    def step2(b):
        moves[b, HA].wait_recv()
        p[b, zrows(1, 0), :] += h[b, 0]
        rsend(b, RMA, p.at[b, zrows(1, 0)], rm.at[b, 0], z_up)
        moves[b, HB].wait_recv()
        p[b, zrows(3, 1), :] += h[b, 1]
        rsend(b, RPB, p.at[b, zrows(3, 1)], rp.at[b, 1], z_dn)

    def zsum(b, part):
        p[b, zrows(0, part), :] += rm[b, part] + rp[b, part]

    def step3(b):
        for role in (RMB, RPA, RMA, RPB):
            moves[b, role].wait_recv()
        p[b, zrows(0, 1 - hx), :] += rm[b, 1 - hx] + rp[b, 1 - hx]
        rsend(b, XH, p.at[b, zrows(0, 1 - hx)], xb.at[b], x_hi)
        p[b, zrows(0, hx), :] += rm[b, hx] + rp[b, hx]

    source = [
        dp, (dp + 4) % 8,
        xl * 4 + (y + 1) % 4, xl * 4 + (y + 3) % 4, xl * 4 + (y + 2) % 4,
        (1 - xl) * 4 + (y + 1) % 4, (1 - xl) * 4 + (y + 3) % 4, (1 - xl) * 4 + (y + 2) % 4,
    ]

    def step4(b):
        moves[b, XH].wait_recv()
        total = p[b, zrows(0, hx), :] + xb[b]
        prod = total[:, :128] * total[:, 128:]
        prod = jnp.concatenate([prod, jnp.zeros((128 - CH, 128), F32)], axis=0)
        row = lax.broadcasted_iota(jnp.int32, (32, 128), 0)
        col = lax.broadcasted_iota(jnp.int32, (32, 128), 1)
        pick = (row == source[b] * 4 + col // RANK).astype(F32)
        acc[...] += nt(pick, prod)

    acc[...] = jnp.zeros_like(acc)
    mm(0)
    step1(0)
    step2(0)
    step3(0)

    q3.wait_recv()
    q4a = qsend(3, 3, 4, lo, y_up)
    q2.wait_recv()
    q4b = qsend(4, 2, 4, hi, y_dn)
    q1.wait_recv()
    q6 = qsend(5, 1, 6, full, y_up)
    q5 = qsend(6, 1, 5, full, y_dn)
    mm(1)
    mm(2)
    step1(1)
    mm(3)
    step1(2)
    step2(1)
    step1(3)
    step2(2)
    step3(1)
    q4a.wait_recv()
    q4b.wait_recv()
    mm(4)
    step4(0)
    step1(4)
    step2(3)
    step3(2)
    step4(1)
    step2(4)
    step3(3)
    q6.wait_recv()
    q7a = qsend(7, 6, 7, lo, y_up)
    q5.wait_recv()
    q7b = qsend(8, 5, 7, hi, y_dn)
    mm(5)
    mm(6)
    step1(5)
    step3(4)
    step4(2)
    step1(6)
    step2(5)
    q7a.wait_recv()
    q7b.wait_recv()
    mm(7)
    step2(6)
    step1(7)
    step3(5)
    step4(3)
    step2(7)
    step3(6)
    step4(4)
    step3(7)
    step4(5)
    step4(6)
    step4(7)

    slot = c * 8 + z * 2 + hx
    mine = acc[...] * F32(RANK ** -0.5)
    seen = ids[pl.ds(slot, 1), :]
    doc = lax.broadcasted_iota(jnp.int32, (128, 128), 0)
    sums = nt(mine, (doc == seen).astype(F32))
    counts = nt(jnp.ones((32, 128), F32), (doc - 64 == seen).astype(F32))
    msg[pl.ds(0, 32), :] = mine
    msg[pl.ds(32, 32), :] = sums + counts
    g[slot] = msg[...]
    got = []
    for k in range(1, 16):
        to = {"dp": dp, "tensor": (t + k) % 16}
        got.append(send(msg, g.at[slot], gs.at[k - 1], gr.at[k - 1], to))
    for cp in got:
        cp.wait_recv()
    part = g[0, pl.ds(32, 32), :]
    for m in range(1, 16):
        part = part + g[m, pl.ds(32, 32), :]
    dpb[dp] = part
    got = []
    for k in range(1, 8):
        to = {"dp": (dp + k) % 8, "tensor": t}
        got.append(send(dpb.at[dp], dpb.at[dp], ds_.at[k - 1], dr.at[k - 1], to))
    scores_out[...] = jnp.concatenate([g[m, pl.ds(0, 32), :][:, :CH] for m in range(16)], axis=1)
    for cp in got:
        cp.wait_recv()
    whole = dpb[0]
    for m in range(1, 8):
        whole = whole + dpb[m]
    docs_out[...] = (whole / pltpu.roll(whole, 64, 1))[:, :64]
    for cp in sent:
        cp.wait_send()


def body(activations, deltas, query_in, query_out, doc_ids):
    ids = jnp.pad(doc_ids.reshape(16, CH), ((0, 0), (0, 128 - CH)), constant_values=-1000)
    any_ = pl.BlockSpec(memory_space=pl.ANY)
    vmem = pl.BlockSpec(memory_space=pltpu.VMEM)
    dma = pltpu.SemaphoreType.DMA
    scores, docs = pl.pallas_call(
        kernel,
        out_shape=(
            jax.ShapeDtypeStruct((32, ROWS), F32),
            jax.ShapeDtypeStruct((32, 64), F32),
        ),
        in_specs=[any_, any_, any_, any_, vmem],
        out_specs=(vmem, vmem),
        scratch_shapes=[
            pltpu.VMEM((ROWS, KIN), jnp.bfloat16),
            pltpu.VMEM((ROWS, KOUT), jnp.bfloat16),
            pltpu.VMEM((NB, K, 128), jnp.bfloat16),
            pltpu.VMEM((NB, ROWS, 256), F32),
            pltpu.VMEM((NB, HALF, 256), F32),
            pltpu.VMEM((NB, 2, CH, 256), F32),
            pltpu.VMEM((NB, 2, CH, 256), F32),
            pltpu.VMEM((NB, 2, CH, 256), F32),
            pltpu.VMEM((NB, CH, 256), F32),
            pltpu.VMEM((32, 128), F32),
            pltpu.VMEM((64, 128), F32),
            pltpu.VMEM((16, 64, 128), F32),
            pltpu.VMEM((8, 32, 128), F32),
            dma((4,)), dma((9,)), dma((9,)), dma((8, NB)), dma((8, NB)),
            dma((15,)), dma((15,)), dma((7,)), dma((7,)),
        ],
        compiler_params=pltpu.CompilerParams(
            collective_id=0, has_side_effects=True, vmem_limit_bytes=60 * 1024 * 1024
        ),
    )(activations, deltas, query_in, query_out, ids)
    return scores.T, docs.T


def solution(mesh):
    return jax.shard_map(
        body,
        mesh=mesh,
        in_specs=(
            P("dp", "tensor"),
            P("dp", "tensor"),
            P("tensor", "dp"),
            P("tensor", "dp"),
            P("dp"),
        ),
        out_specs=(P("dp", None), P()),
        check_vma=False,
    )
```

time: 283 us -> 106 us (0.37)
  waiting for transfers between devices: 194 us -> 0 us
  Pallas kernels: 0 us -> 101 us
  matrix products: 20.8 us -> 0 us
  local copies, waits for them, and re-layouts: 20.8 us -> 4.31 us
  between operations: 16.1 us -> 0.64 us
  other arithmetic: 14.4 us -> 0 us
  blocking collectives: 9.83 us -> 0 us
  starting transfers between devices: 5.07 us -> 0 us
    unnamed x3 -> x0, waiting for transfers between devices: 124 us -> none
    pallas_call x0 -> x1, Pallas kernels: none -> 101 us  [body(): pl.pallas_call(kernel, out_shape=(jax.ShapeDtypeStruct((32, ROWS), F32),...]
    all_gather x1 -> x0, waiting for transfers between devices: 63.1 us -> none  [side_by_side(): filled, at, done = (lax.all_gather(both, axis, axis=dim, tiled=True), 0, [])]
    dot_general x3 -> x0, matrix products: 20.8 us -> none  [the longest x1 10.9 us: body(): proj_out = jnp.dot(deltas, full_out, preferred_element_type=jnp.float32)]
    concatenate x3 -> x0, other arithmetic: 12.5 us -> none  [the longest x1 10.4 us: sent_together(): both = jnp.concatenate(arrays, axis=along)]
    unnamed x10 -> x2, local copies, waits for them, and re-layouts: 14.5 us -> 2.94 us
    all_to_all x1 -> x0, blocking collectives: 9.83 us -> none  [copy_for_each(): return lax.all_to_all(copies, axis, split_axis=0, concat_axis=0, tiled=True)]
    all_to_all x1 -> x0, waiting for transfers between devices: 7.38 us -> none  [copy_for_each(): return lax.all_to_all(copies, axis, split_axis=0, concat_axis=0, tiled=True)]
  transfers between devices with their start and end apart: 3 -> 0, of which waited for: 3 -> 0; matrix products, arithmetic and copies ran while one was open for 1% -> 0% of each run, Pallas kernels for 0% -> 0%
where the time goes in v1:
time: 106 us
  Pallas kernels  101 us (95%)
  local copies, waits for them, and re-layouts  4.31 us (4%)
    pallas_call x1, Pallas kernels, body(): pl.pallas_call(kernel, out_shape=(jax.ShapeDtypeStruct((32, ROWS), F32),...  101 us
    unnamed x2, local copies, waits for them, and re-layouts  2.94 us

profile of v1, /device:TPU:1, one launch (start us, length us, event | category | flops | bytes accessed | tf_op | source)
XLA Modules:
  0.0 105.6 jit_solution(4913679238063717177)
XLA Ops:
  0.6 0.8 reshape.7
  1.4 0.6 pad.4.ids
  2.0 100.6 %shard_map.68 = (f32[32,1536]{1,0:T(8,128)}, f32[32,64]{1,0:T(8,128)}) custom-call(bf16[1536,512]{1,0:T(8,128)(2,1)} %act.1, bf16[1536,1792]{1,0:T(8,128)(2,1)} %dl.1, bf16[512,128]{1,0:T(8,128)(2,1)} %qi.1, bf16[1792,128]{1,0:T(8,128)(2,1)} %qo.1, s32[16,128]{1,0:T(8,128)} %pad.4.ids), custom_call_target="tpu_custom_call" | custom-call | tf_op jit(solution)/shard_map/pallas_call | solution.py:262
  102.6 1.6 %copy.9 = f32[1536,32]{0,1:T(8,128)} copy(f32[1536,32]{0,1:T(8,128)} %bitcast.2) | data formatting | bytes 393216
  104.3 1.3 %copy.10 = f32[64,32]{0,1:T(8,128)} copy(f32[64,32]{0,1:T(8,128)} %bitcast.3) | data formatting | bytes 16384

commit v2 on v1

v2 whole, which is shorter than its diff:
```python
import jax
import jax.numpy as jnp
from jax import lax
from jax.experimental import pallas as pl
from jax.experimental.pallas import tpu as pltpu
from jax.sharding import PartitionSpec as P

RANK = 32
MESH = pl.DeviceIdType.MESH
F32 = jnp.float32
HIGHEST = lax.Precision.HIGHEST

ROWS = 1536
HALF = ROWS // 2
ZCH = HALF // 4
CH = ZCH // 2
KIN = 512
KOUT = 1792
K = KIN + KOUT
KH = K // 2
NB = 8
TM = 256
HA, HB, RMA, RMB, RPA, RPB, XH, D2D = range(8)
GR = 16
CR = CH + GR
UNIT = 32704.0


def nt(a, b):
    return lax.dot_general(
        a, b, (((1,), (1,)), ((), ())), precision=HIGHEST, preferred_element_type=F32
    )


def enc(x):
    codes, tops = [], []
    for i in range(CH // GR):
        part = x[i * GR : (i + 1) * GR]
        top = jnp.maximum(jnp.max(jnp.abs(part), axis=0, keepdims=True), F32(2.0**-110))
        top = jnp.ceil(jnp.log2(top))
        codes.append(jnp.round(part * (jnp.exp2(-top) * F32(UNIT))))
        tops.append(top)
    tops.append(jnp.zeros((GR - CH // GR, x.shape[1]), F32))
    rows = codes + [jnp.concatenate(tops, axis=0)]
    return jnp.concatenate(rows, axis=0).astype(jnp.int32).astype(jnp.int16)


def dec(m):
    tops = m[CH:].astype(jnp.int32).astype(F32)
    tops = jnp.exp2(tops) * F32(1.0 / UNIT)
    out = []
    for i in range(CH // GR):
        part = m[i * GR : (i + 1) * GR].astype(jnp.int32).astype(F32)
        out.append(part * tops[i : i + 1])
    return jnp.concatenate(out, axis=0)


def kernel(
    act, dl, qi, qo, ids, scores_out, docs_out,
    a_in, a_out, q, p, dbuf, sb, rb, fin, acc, cnt, oh, msga, msgb, ga, gb, dpa, dpb,
    lsem, qs, qr, rs, rr, gs, gr, ds_, dr,
):
    dp = lax.axis_index("dp")
    t = lax.axis_index("tensor")
    xl, y = dp // 4, dp % 4
    hx, z, c = t // 8, (t // 2) % 4, t % 2

    x_lo = {"dp": (dp + 4) % 8, "tensor": t}
    y_up = {"dp": xl * 4 + (y + 1) % 4, "tensor": t}
    y_dn = {"dp": xl * 4 + (y + 3) % 4, "tensor": t}
    x_hi = {"dp": dp, "tensor": (t + 8) % 16}
    z_up = {"dp": dp, "tensor": hx * 8 + ((z + 1) % 4) * 2 + c}
    z_dn = {"dp": dp, "tensor": hx * 8 + ((z + 3) % 4) * 2 + c}
    mate = {"dp": dp, "tensor": hx * 8 + z * 2 + 1 - c}

    loads = [
        pltpu.make_async_copy(qi, q.at[0, pl.ds(0, KIN)], lsem.at[0]),
        pltpu.make_async_copy(qo, q.at[0, pl.ds(KIN, KOUT)], lsem.at[1]),
        pltpu.make_async_copy(act, a_in, lsem.at[2]),
        pltpu.make_async_copy(dl, a_out, lsem.at[3]),
    ]
    for cp in loads:
        cp.start()

    barrier = pltpu.get_barrier_semaphore()
    for k in range(1, 16):
        pl.semaphore_signal(
            barrier, inc=1, device_id={"dp": dp, "tensor": (t + k) % 16}, device_id_type=MESH
        )
    for k in range(1, 8):
        pl.semaphore_signal(
            barrier, inc=1, device_id={"dp": (dp + k) % 8, "tensor": t}, device_id_type=MESH
        )

    slot = c * 8 + z * 2 + hx
    at = slot * CH
    line, off = at // 128, at % 128
    one = jnp.broadcast_to(ids[pl.ds(line, 1), :], (8, 128))
    two = jnp.broadcast_to(ids[pl.ds(jnp.minimum(line + 1, ROWS // 128 - 1), 1), :], (8, 128))
    lane = lax.broadcasted_iota(jnp.int32, (8, 128), 1)
    turn = (128 - off) % 128
    seen = jnp.where(lane < 128 - off, pltpu.roll(one, turn, 1), pltpu.roll(two, turn, 1))
    seen = jnp.where(lane < CH, seen, -1000)[:1]
    doc = lax.broadcasted_iota(jnp.int32, (128, 128), 0)
    oh[...] = (doc == seen).astype(F32)
    cnt[...] = nt(jnp.ones((8, 128), F32), (doc - 64 == seen).astype(F32))

    pl.semaphore_wait(barrier, 22)

    sent = []

    def send(src, dst, ss, rsem, to):
        cp = pltpu.make_async_remote_copy(
            src_ref=src, dst_ref=dst, send_sem=ss, recv_sem=rsem,
            device_id=to, device_id_type=MESH,
        )
        cp.start()
        sent.append(cp)
        return cp

    lo, hi, full = pl.ds(0, KH), pl.ds(KH, KH), pl.ds(0, K)

    def qsend(n, src, dst, rows, to):
        return send(q.at[src, rows], q.at[dst, rows], qs.at[n], qr.at[n], to)

    loads[0].wait()
    loads[1].wait()
    q1 = qsend(0, 0, 1, full, x_lo)
    q3 = qsend(1, 0, 3, full, y_up)
    q2 = qsend(2, 0, 2, full, y_dn)
    loads[2].wait()
    loads[3].wait()

    moves = {}

    def rsend(b, role, src, dst, to):
        moves[b, role] = send(src, dst, rs.at[role, b], rr.at[role, b], to)

    own, other = c * HALF, (1 - c) * HALF

    def code(b, role, x, to):
        sb[b, role] = enc(x)
        rsend(b, role, sb.at[b, role], rb.at[b, role], to)

    def chip(b, dz, part):
        rel = ((z + dz) % 4) * ZCH + part * CH
        rows = pl.ds(pl.multiple_of(own + rel, CH), CH)
        return p[b, rows, :] + dbuf[b, pl.ds(pl.multiple_of(rel, CH), CH), :]

    def mm(*bs):
        for base in (other, own):

            def tile(i, carry, base=base):
                rows = pl.ds(pl.multiple_of(base + i * TM, TM), TM)
                for lhs, first, deep, col in ((a_in, 0, KIN, 0), (a_out, KIN, KOUT, 128)):
                    rhs = [q[b, pl.ds(first, deep), :] for b in bs]
                    rhs = rhs[0] if len(bs) == 1 else jnp.concatenate(rhs, axis=1)
                    out = jnp.dot(lhs[rows, :], rhs, preferred_element_type=F32)
                    for i, b in enumerate(bs):
                        p[b, rows, pl.ds(col, 128)] = out[:, i * 128 : (i + 1) * 128]
                return carry

            lax.fori_loop(0, HALF // TM, tile, 0)
            if base is other:
                for b in bs:
                    rows = pl.ds(pl.multiple_of(other, HALF), HALF)
                    rsend(b, D2D, p.at[b, rows], dbuf.at[b], mate)

    def s1(b):
        moves[b, D2D].wait_recv()
        code(b, HA, chip(b, 2, 0), z_up)
        code(b, HB, chip(b, 2, 1), z_dn)
        code(b, RMB, chip(b, 1, 1), z_up)
        code(b, RPA, chip(b, 3, 0), z_dn)

    def s2(b):
        moves[b, HA].wait_recv()
        code(b, RMA, chip(b, 1, 0) + dec(rb[b, HA]), z_up)
        moves[b, HB].wait_recv()
        code(b, RPB, chip(b, 3, 1) + dec(rb[b, HB]), z_dn)

    def s3(b):
        for role in (RMB, RPA, RMA, RPB):
            moves[b, role].wait_recv()
        far = 1 - hx
        code(b, XH, chip(b, 0, far) + dec(rb[b, RMA + far]) + dec(rb[b, RPA + far]), x_hi)
        fin[b] = chip(b, 0, hx) + dec(rb[b, RMA + hx]) + dec(rb[b, RPA + hx])

    source = [
        dp, (dp + 4) % 8,
        xl * 4 + (y + 1) % 4, xl * 4 + (y + 3) % 4, xl * 4 + (y + 2) % 4,
        (1 - xl) * 4 + (y + 1) % 4, (1 - xl) * 4 + (y + 3) % 4, (1 - xl) * 4 + (y + 2) % 4,
    ]

    def s4(b):
        moves[b, XH].wait_recv()
        total = fin[b] + dec(rb[b, XH])
        prod = total[:, :128] * total[:, 128:]
        prod = jnp.concatenate([prod, jnp.zeros((128 - CH, 128), F32)], axis=0)
        row = lax.broadcasted_iota(jnp.int32, (8, 128), 0)
        col = lax.broadcasted_iota(jnp.int32, (8, 128), 1)
        pick = jnp.where(row == (b % 2) * 4 + col // RANK, F32(RANK ** -0.5), F32(0))
        acc[b] = nt(pick, prod)

    def share(first, last, msg, g, n):
        rows = (last - first) * 4
        for b in range(first, last, 2):
            msg[pl.ds((b - first) * 4, 8), :] = acc[b] + acc[b + 1]
        mine = msg[pl.ds(0, rows), :]
        msg[pl.ds(rows, rows), :] = nt(mine, oh[...]) + jnp.broadcast_to(cnt[:1], (rows, 128))
        g[slot] = msg[...]
        got = []
        for k in range(1, 16):
            to = {"dp": dp, "tensor": (t + k) % 16}
            got.append(send(msg, g.at[slot], gs.at[n, k - 1], gr.at[n, k - 1], to))
        return got

    def rows_of(first, last, found, out, source=source):
        row = lax.broadcasted_iota(jnp.int32, out.shape, 0)
        for b in range(first, last):
            for j in range(4):
                i = (b - first) * 4 + j
                line = jnp.broadcast_to(found[i : i + 1], out.shape)
                out = jnp.where(row == source[b] * 4 + j, line, out)
        return out

    def total(got, g, buf, n, spread):
        for cp in got:
            cp.wait_recv()
        rows = g.shape[1] // 2
        part = g[0, pl.ds(rows, rows), :]
        for m in range(1, 16):
            part = part + g[m, pl.ds(rows, rows), :]
        buf[dp] = spread(part)
        got = []
        for k in range(1, 8):
            to = {"dp": (dp + k) % 8, "tensor": t}
            got.append(send(buf.at[dp], buf.at[dp], ds_.at[n, k - 1], dr.at[n, k - 1], to))
        return got

    def place(first, last, g):
        rows = (last - first) * 4
        found = jnp.concatenate([g[m, pl.ds(0, rows), :][:, :CH] for m in range(16)], axis=1)
        old = jnp.zeros((32, ROWS), F32) if first == 0 else scores_out[...]
        scores_out[...] = rows_of(first, last, found, old)

    def mean(early, late):
        for cp in early:
            cp.wait_recv()
        whole = dpa[0]
        for m in range(1, 8):
            whole = whole + dpa[m]
        for cp in late:
            cp.wait_recv()
        for m in range(8):
            where = [(1 - m // 4) * 4 + (m + 3) % 4, (1 - m // 4) * 4 + (m + 2) % 4]
            whole = whole + rows_of(0, 2, dpb[m], jnp.zeros((32, 128), F32), where)
        docs_out[...] = (whole / pltpu.roll(whole, 64, 1))[:, :64]

    mm(0)
    s1(0)
    s2(0)
    s3(0)

    q3.wait_recv()
    q4a = qsend(3, 3, 4, lo, y_up)
    q2.wait_recv()
    q4b = qsend(4, 2, 4, hi, y_dn)
    q5a = qsend(5, 2, 5, lo, x_lo)
    q5b = qsend(6, 2, 5, hi, x_lo)
    q1.wait_recv()
    q6 = qsend(7, 1, 6, full, y_up)
    mm(1, 2)
    s1(1)
    s1(2)
    mm(3)
    q5a.wait_recv()
    q7a = qsend(8, 5, 7, lo, y_dn)
    s2(1)
    s1(3)
    s2(2)
    s4(0)
    q4a.wait_recv()
    q4b.wait_recv()
    mm(4)
    s3(1)
    s2(3)
    s1(4)
    s3(2)
    q5b.wait_recv()
    q7b = qsend(9, 5, 7, hi, y_dn)
    mm(5)
    s4(1)
    s3(3)
    s2(4)
    s1(5)
    s4(2)
    s3(4)
    s2(5)
    s4(3)
    s4(4)
    s3(5)
    q6.wait_recv()
    q7a.wait_recv()
    q7b.wait_recv()
    mm(6, 7)
    s4(5)
    share_a = share(0, 6, msga, ga, 0)
    s1(6)
    s1(7)
    s2(6)
    s2(7)
    total_a = total(share_a, ga, dpa, 0, lambda v: rows_of(0, 6, v, jnp.zeros((32, 128), F32)))
    s3(6)
    s3(7)
    place(0, 6, ga)
    s4(6)
    s4(7)
    share_b = share(6, 8, msgb, gb, 1)
    total_b = total(share_b, gb, dpb, 1, lambda v: v)
    place(6, 8, gb)
    mean(total_a, total_b)
    for cp in sent:
        cp.wait_send()


def body(activations, deltas, query_in, query_out, doc_ids):
    ids = doc_ids.reshape(ROWS // 128, 128)
    any_ = pl.BlockSpec(memory_space=pl.ANY)
    vmem = pl.BlockSpec(memory_space=pltpu.VMEM)
    dma = pltpu.SemaphoreType.DMA
    scores, docs = pl.pallas_call(
        kernel,
        out_shape=(
            jax.ShapeDtypeStruct((32, ROWS), F32),
            jax.ShapeDtypeStruct((32, 64), F32),
        ),
        in_specs=[any_, any_, any_, any_, vmem],
        out_specs=(vmem, vmem),
        scratch_shapes=[
            pltpu.VMEM((ROWS, KIN), jnp.bfloat16),
            pltpu.VMEM((ROWS, KOUT), jnp.bfloat16),
            pltpu.VMEM((NB, K, 128), jnp.bfloat16),
            pltpu.VMEM((NB, ROWS, 256), F32),
            pltpu.VMEM((NB, HALF, 256), F32),
            pltpu.VMEM((NB, 7, CR, 256), jnp.int16),
            pltpu.VMEM((NB, 7, CR, 256), jnp.int16),
            pltpu.VMEM((NB, CH, 256), F32),
            pltpu.VMEM((NB, 8, 128), F32),
            pltpu.VMEM((8, 128), F32),
            pltpu.VMEM((128, 128), F32),
            pltpu.VMEM((48, 128), F32),
            pltpu.VMEM((16, 128), F32),
            pltpu.VMEM((16, 48, 128), F32),
            pltpu.VMEM((16, 16, 128), F32),
            pltpu.VMEM((8, 32, 128), F32),
            pltpu.VMEM((8, 8, 128), F32),
            dma((4,)), dma((10,)), dma((10,)), dma((8, NB)), dma((8, NB)),
            dma((2, 15)), dma((2, 15)), dma((2, 7)), dma((2, 7)),
        ],
        compiler_params=pltpu.CompilerParams(
            collective_id=0, has_side_effects=True, vmem_limit_bytes=60 * 1024 * 1024
        ),
    )(activations, deltas, query_in, query_out, ids)
    return scores.T, docs.T


def solution(mesh):
    return jax.shard_map(
        body,
        mesh=mesh,
        in_specs=(
            P("dp", "tensor"),
            P("dp", "tensor"),
            P("tensor", "dp"),
            P("tensor", "dp"),
            P("dp"),
        ),
        out_specs=(P("dp", None), P()),
        check_vma=False,
    )
```

time: 106 us -> 91.3 us (0.86)
  Pallas kernels: 101 us -> 87.5 us
  local copies, waits for them, and re-layouts: 4.31 us -> 2.94 us
    pallas_call x1, Pallas kernels: 101 us -> 87.5 us  [body(): pl.pallas_call(kernel, out_shape=(jax.ShapeDtypeStruct((32, ROWS), F32),...]
where the time goes in v2:
time: 91.3 us; the launch traced here: 91.1 us
  Pallas kernels  87.5 us (96%)
  local copies, waits for them, and re-layouts  2.94 us (3%)
    pallas_call x1, Pallas kernels, body(): pl.pallas_call(kernel, out_shape=(jax.ShapeDtypeStruct((32, ROWS), F32),...  87.5 us
    unnamed x2, local copies, waits for them, and re-layouts  2.94 us

profile of v2, /device:TPU:1, one launch (start us, length us, event | category | flops | bytes accessed | tf_op | source)
XLA Modules:
  0.0 91.1 jit_solution(9424103330439222506)
XLA Ops:
  0.6 87.5 %shard_map.68 = (f32[32,1536]{1,0:T(8,128)}, f32[32,64]{1,0:T(8,128)}) custom-call(bf16[1536,512]{1,0:T(8,128)(2,1)} %act.1, bf16[1536,1792]{1,0:T(8,128)(2,1)} %dl.1, bf16[512,128]{1,0:T(8,128)(2,1)} %qi.1, bf16[1792,128]{1,0:T(8,128)(2,1)} %qo.1, s32[12,128]{1,0:T(8,128)} %bitcast.5), custom_call_target="tpu_custom_call" | custom-call | tf_op jit(solution)/shard_map/pallas_call | solution.py:332
  88.1 1.6 %copy.9 = f32[1536,32]{0,1:T(8,128)} copy(f32[1536,32]{0,1:T(8,128)} %bitcast.3) | data formatting | bytes 393216
  89.7 1.3 %copy.10 = f32[64,32]{0,1:T(8,128)} copy(f32[64,32]{0,1:T(8,128)} %bitcast.4) | data formatting | bytes 16384

commit v3 on v2

--- a/solution.py
+++ b/solution.py
@@ -20,7 +20,8 @@
 KH = K // 2
 NB = 8
 TM = 256
-HA, HB, RMA, RMB, RPA, RPB, XH, D2D = range(8)
+HA, HB, RMA, RMB, RPA, RPB, XH = range(7)
+KQ = K // 4
 GR = 16
 CR = CH + GR
 UNIT = 32704.0
@@ -57,8 +58,8 @@
 
 def kernel(
     act, dl, qi, qo, ids, scores_out, docs_out,
-    a_in, a_out, q, p, dbuf, sb, rb, fin, acc, cnt, oh, msga, msgb, ga, gb, dpa, dpb,
-    lsem, qs, qr, rs, rr, gs, gr, ds_, dr,
+    a_in, a_out, q, p, dbuf, sb, rb, fin, acc, cnt, oh, every, msga, msgb, ga, gb, dpa, dpb,
+    lsem, qs, qr, rs, rr, ms, mr, gs, gr, ds_, dr,
 ):
     dp = lax.axis_index("dp")
     t = lax.axis_index("tensor")
@@ -104,6 +105,9 @@
     doc = lax.broadcasted_iota(jnp.int32, (128, 128), 0)
     oh[...] = (doc == seen).astype(F32)
     cnt[...] = nt(jnp.ones((8, 128), F32), (doc - 64 == seen).astype(F32))
+    for i in range(ROWS // 128):
+        group = ids[pl.ds(i, 1), :]
+        every[:, pl.ds(i * 128, 128)] = (doc == group).astype(jnp.bfloat16)
 
     pl.semaphore_wait(barrier, 22)
 
@@ -118,16 +122,20 @@
         sent.append(cp)
         return cp
 
-    lo, hi, full = pl.ds(0, KH), pl.ds(KH, KH), pl.ds(0, K)
+    lo, hi = pl.ds(0, KH), pl.ds(KH, KH)
+    quarter = [pl.ds(i * KQ, KQ) for i in (2, 3, 0, 1)]
 
     def qsend(n, src, dst, rows, to):
         return send(q.at[src, rows], q.at[dst, rows], qs.at[n], qr.at[n], to)
 
     loads[0].wait()
     loads[1].wait()
-    q1 = qsend(0, 0, 1, full, x_lo)
-    q3 = qsend(1, 0, 3, full, y_up)
-    q2 = qsend(2, 0, 2, full, y_dn)
+    q1a = qsend(0, 0, 1, lo, x_lo)
+    q3a = qsend(1, 0, 3, lo, y_up)
+    q2b = qsend(2, 0, 2, hi, y_dn)
+    q1b = qsend(3, 0, 1, hi, x_lo)
+    q3b = qsend(4, 0, 3, hi, y_up)
+    q2a = qsend(5, 0, 2, lo, y_dn)
     loads[2].wait()
     loads[3].wait()
 
@@ -147,27 +155,49 @@
         rows = pl.ds(pl.multiple_of(own + rel, CH), CH)
         return p[b, rows, :] + dbuf[b, pl.ds(pl.multiple_of(rel, CH), CH), :]
 
+    def tile(bs, rows):
+        for lhs, first, deep, col in ((a_in, 0, KIN, 0), (a_out, KIN, KOUT, 128)):
+            rhs = [q[b, pl.ds(first, deep), :] for b in bs]
+            rhs = rhs[0] if len(bs) == 1 else jnp.concatenate(rhs, axis=1)
+            out = jnp.dot(lhs[rows, :], rhs, preferred_element_type=F32)
+            for i, b in enumerate(bs):
+                p[b, rows, pl.ds(col, 128)] = out[:, i * 128 : (i + 1) * 128]
+
+    pieces = HALF // TM
+
+    def piece(b, i, start=False):
+        rows = pl.ds(pl.multiple_of(other + i * TM, TM), TM)
+        cp = pltpu.make_async_remote_copy(
+            src_ref=p.at[b, rows],
+            dst_ref=dbuf.at[b, pl.ds(pl.multiple_of(i * TM, TM), TM)],
+            send_sem=ms.at[b, i], recv_sem=mr.at[b, i],
+            device_id=mate, device_id_type=MESH,
+        )
+        if start:
+            cp.start()
+        return cp
+
     def mm(*bs):
-        for base in (other, own):
-
-            def tile(i, carry, base=base):
-                rows = pl.ds(pl.multiple_of(base + i * TM, TM), TM)
-                for lhs, first, deep, col in ((a_in, 0, KIN, 0), (a_out, KIN, KOUT, 128)):
-                    rhs = [q[b, pl.ds(first, deep), :] for b in bs]
-                    rhs = rhs[0] if len(bs) == 1 else jnp.concatenate(rhs, axis=1)
-                    out = jnp.dot(lhs[rows, :], rhs, preferred_element_type=F32)
-                    for i, b in enumerate(bs):
-                        p[b, rows, pl.ds(col, 128)] = out[:, i * 128 : (i + 1) * 128]
-                return carry
-
-            lax.fori_loop(0, HALF // TM, tile, 0)
-            if base is other:
-                for b in bs:
-                    rows = pl.ds(pl.multiple_of(other, HALF), HALF)
-                    rsend(b, D2D, p.at[b, rows], dbuf.at[b], mate)
+        def first(i, carry):
+            tile(bs, pl.ds(pl.multiple_of(other + i * TM, TM), TM))
+            for b in bs:
+                piece(b, i, True)
+            return carry
+
+        def rest(i, carry):
+            tile(bs, pl.ds(pl.multiple_of(own + i * TM, TM), TM))
+            return carry
+
+        lax.fori_loop(0, pieces, first, 0)
+        lax.fori_loop(0, pieces, rest, 0)
+        for b in bs:
+            for i in range(pieces):
+                moves[b, "core", i] = piece(b, i)
+                sent.append(moves[b, "core", i])
 
     def s1(b):
-        moves[b, D2D].wait_recv()
+        for i in range(pieces):
+            moves[b, "core", i].wait_recv()
         code(b, HA, chip(b, 2, 0), z_up)
         code(b, HB, chip(b, 2, 1), z_dn)
         code(b, RMB, chip(b, 1, 1), z_up)
@@ -202,18 +232,24 @@
         pick = jnp.where(row == (b % 2) * 4 + col // RANK, F32(RANK ** -0.5), F32(0))
         acc[b] = nt(pick, prod)
 
-    def share(first, last, msg, g, n):
-        rows = (last - first) * 4
-        for b in range(first, last, 2):
-            msg[pl.ds((b - first) * 4, 8), :] = acc[b] + acc[b + 1]
-        mine = msg[pl.ds(0, rows), :]
-        msg[pl.ds(rows, rows), :] = nt(mine, oh[...]) + jnp.broadcast_to(cnt[:1], (rows, 128))
+    def spread(msg, g, n):
         g[slot] = msg[...]
         got = []
         for k in range(1, 16):
             to = {"dp": dp, "tensor": (t + k) % 16}
             got.append(send(msg, g.at[slot], gs.at[n, k - 1], gr.at[n, k - 1], to))
         return got
+
+    def share_a():
+        for b in range(0, 6, 2):
+            msga[pl.ds(b * 4, 8), :] = acc[b] + acc[b + 1]
+        return spread(msga, ga, 0)
+
+    def share_b():
+        mine = acc[6] + acc[7]
+        msgb[pl.ds(0, 8), :] = mine
+        msgb[pl.ds(8, 8), :] = nt(mine, oh[...]) + cnt[...]
+        return spread(msgb, gb, 1)
 
     def rows_of(first, last, found, out, source=source):
         row = lax.broadcasted_iota(jnp.int32, out.shape, 0)
@@ -224,25 +260,40 @@
                 out = jnp.where(row == source[b] * 4 + j, line, out)
         return out
 
-    def total(got, g, buf, n, spread):
+    def gathered(g, rows):
+        return jnp.concatenate([g[m, pl.ds(0, rows), :][:, :CH] for m in range(16)], axis=1)
+
+    def finish_a(got):
         for cp in got:
             cp.wait_recv()
-        rows = g.shape[1] // 2
-        part = g[0, pl.ds(rows, rows), :]
+        found = gathered(ga, 24)
+        scores_out[...] = rows_of(0, 6, found, jnp.zeros((32, ROWS), F32))
+        one = found.astype(jnp.bfloat16)
+        left = found - one.astype(F32)
+        two = left.astype(jnp.bfloat16)
+        three = (left - two.astype(F32)).astype(jnp.bfloat16)
+        sums = jnp.zeros((24, 128), F32)
+        for part in (three, two, one):
+            sums = sums + lax.dot_general(
+                part, every[...], (((1,), (1,)), ((), ())), preferred_element_type=F32
+            )
+        return across(dpa, rows_of(0, 6, sums, jnp.zeros((32, 128), F32)), 0)
+
+    def finish_b(got):
+        for cp in got:
+            cp.wait_recv()
+        part = gb[0, pl.ds(8, 8), :]
         for m in range(1, 16):
-            part = part + g[m, pl.ds(rows, rows), :]
-        buf[dp] = spread(part)
+            part = part + gb[m, pl.ds(8, 8), :]
+        return across(dpb, part, 1)
+
+    def across(buf, part, n):
+        buf[dp] = part
         got = []
         for k in range(1, 8):
             to = {"dp": (dp + k) % 8, "tensor": t}
             got.append(send(buf.at[dp], buf.at[dp], ds_.at[n, k - 1], dr.at[n, k - 1], to))
         return got
-
-    def place(first, last, g):
-        rows = (last - first) * 4
-        found = jnp.concatenate([g[m, pl.ds(0, rows), :][:, :CH] for m in range(16)], axis=1)
-        old = jnp.zeros((32, ROWS), F32) if first == 0 else scores_out[...]
-        scores_out[...] = rows_of(first, last, found, old)
 
     def mean(early, late):
         for cp in early:
@@ -255,71 +306,81 @@
         for m in range(8):
             where = [(1 - m // 4) * 4 + (m + 3) % 4, (1 - m // 4) * 4 + (m + 2) % 4]
             whole = whole + rows_of(0, 2, dpb[m], jnp.zeros((32, 128), F32), where)
-        docs_out[...] = (whole / pltpu.roll(whole, 64, 1))[:, :64]
+        held = dpb[0, pl.ds(0, 1), :]
+        for m in range(1, 8):
+            held = held + dpb[m, pl.ds(0, 1), :]
+        held = jnp.broadcast_to(pltpu.roll(jnp.broadcast_to(held, (8, 128)), 64, 1)[:1], (32, 128))
+        docs_out[...] = (whole / held)[:, :64]
+
+    def forward(n):
+        q5[n].wait_recv()
+        q7.append(qsend(14 + n, 5, 7, quarter[n], y_dn))
 
     mm(0)
     s1(0)
     s2(0)
+    q3a.wait_recv()
+    q4a = qsend(6, 3, 4, lo, y_up)
+    q2b.wait_recv()
+    q4b = qsend(7, 2, 4, hi, y_dn)
+    q5 = [qsend(10, 2, 5, quarter[0], x_lo), qsend(11, 2, 5, quarter[1], x_lo)]
+    q7 = []
+    q1a.wait_recv()
+    q6a = qsend(8, 1, 6, lo, y_up)
     s3(0)
-
-    q3.wait_recv()
-    q4a = qsend(3, 3, 4, lo, y_up)
-    q2.wait_recv()
-    q4b = qsend(4, 2, 4, hi, y_dn)
-    q5a = qsend(5, 2, 5, lo, x_lo)
-    q5b = qsend(6, 2, 5, hi, x_lo)
-    q1.wait_recv()
-    q6 = qsend(7, 1, 6, full, y_up)
+    q2a.wait_recv()
+    q5 += [qsend(12, 2, 5, quarter[2], x_lo), qsend(13, 2, 5, quarter[3], x_lo)]
+    q1b.wait_recv()
+    q6b = qsend(9, 1, 6, hi, y_up)
     mm(1, 2)
+    forward(0)
     s1(1)
     s1(2)
+    q3b.wait_recv()
     mm(3)
-    q5a.wait_recv()
-    q7a = qsend(8, 5, 7, lo, y_dn)
+    forward(1)
     s2(1)
     s1(3)
-    s2(2)
-    s4(0)
+    forward(2)
     q4a.wait_recv()
     q4b.wait_recv()
     mm(4)
+    s2(2)
+    forward(3)
+    s1(4)
     s3(1)
     s2(3)
-    s1(4)
+    mm(5)
     s3(2)
-    q5b.wait_recv()
-    q7b = qsend(9, 5, 7, hi, y_dn)
-    mm(5)
+    s1(5)
+    s4(0)
+    s2(4)
+    s3(3)
+    for cp in (q6a, q6b, *q7):
+        cp.wait_recv()
+    mm(6, 7)
     s4(1)
-    s3(3)
-    s2(4)
-    s1(5)
     s4(2)
+    s2(5)
     s3(4)
-    s2(5)
-    s4(3)
-    s4(4)
-    s3(5)
-    q6.wait_recv()
-    q7a.wait_recv()
-    q7b.wait_recv()
-    mm(6, 7)
-    s4(5)
-    share_a = share(0, 6, msga, ga, 0)
     s1(6)
     s1(7)
+    s4(3)
+    s3(5)
     s2(6)
+    s4(4)
     s2(7)
-    total_a = total(share_a, ga, dpa, 0, lambda v: rows_of(0, 6, v, jnp.zeros((32, 128), F32)))
+    s4(5)
     s3(6)
     s3(7)
-    place(0, 6, ga)
+    shared_a = share_a()
     s4(6)
     s4(7)
-    share_b = share(6, 8, msgb, gb, 1)
-    total_b = total(share_b, gb, dpb, 1, lambda v: v)
-    place(6, 8, gb)
-    mean(total_a, total_b)
+    shared_b = share_b()
+    early = finish_a(shared_a)
+    late = finish_b(shared_b)
+    scores_out[...] = rows_of(6, 8, gathered(gb, 8), scores_out[...])
+    mean(early, late)
     for cp in sent:
         cp.wait_send()
 
@@ -349,19 +410,34 @@
             pltpu.VMEM((NB, 8, 128), F32),
             pltpu.VMEM((8, 128), F32),
             pltpu.VMEM((128, 128), F32),
-            pltpu.VMEM((48, 128), F32),
+            pltpu.VMEM((128, ROWS), jnp.bfloat16),
+            pltpu.VMEM((24, 128), F32),
             pltpu.VMEM((16, 128), F32),
-            pltpu.VMEM((16, 48, 128), F32),
+            pltpu.VMEM((16, 24, 128), F32),
             pltpu.VMEM((16, 16, 128), F32),
             pltpu.VMEM((8, 32, 128), F32),
             pltpu.VMEM((8, 8, 128), F32),
-            dma((4,)), dma((10,)), dma((10,)), dma((8, NB)), dma((8, NB)),
+            dma((4,)), dma((18,)), dma((18,)), dma((7, NB)), dma((7, NB)),
+            dma((NB, HALF // TM)), dma((NB, HALF // TM)),
             dma((2, 15)), dma((2, 15)), dma((2, 7)), dma((2, 7)),
         ],
         compiler_params=pltpu.CompilerParams(
             collective_id=0, has_side_effects=True, vmem_limit_bytes=60 * 1024 * 1024
         ),
     )(activations, deltas, query_in, query_out, ids)
+    def finish(a, b, oa, ob):
+        oa[...] = a[...]
+        ob[...] = b[...]
+
+    scores, docs = pl.pallas_call(
+        finish,
+        out_shape=(
+            jax.ShapeDtypeStruct((32, ROWS), F32),
+            jax.ShapeDtypeStruct((32, 64), F32),
+        ),
+        in_specs=[vmem, vmem],
+        out_specs=(vmem, vmem),
+    )(scores, docs)
     return scores.T, docs.T
 
 

time: 91.3 us -> 79.9 us (0.88)
  Pallas kernels: 87.5 us -> 79.1 us
  local copies, waits for them, and re-layouts: 2.94 us -> 0 us
    pallas_call x1, Pallas kernels: 87.5 us -> 77.5 us  [body(): pl.pallas_call(kernel, out_shape=(jax.ShapeDtypeStruct((32, ROWS), F32),...]
    unnamed x2 -> x0, local copies, waits for them, and re-layouts: 2.94 us -> none
    pallas_call x0 -> x1, Pallas kernels: none -> 1.62 us  [body(): pl.pallas_call(finish, out_shape=(jax.ShapeDtypeStruct((32, ROWS), F32),...]
where the time goes in v3:
time: 79.9 us; the launch traced here: 79.7 us
  Pallas kernels  79.1 us (99%)
    pallas_call x1, Pallas kernels, body(): pl.pallas_call(kernel, out_shape=(jax.ShapeDtypeStruct((32, ROWS), F32),...  77.5 us
    pallas_call x1, Pallas kernels, body(): pl.pallas_call(finish, out_shape=(jax.ShapeDtypeStruct((32, ROWS), F32),...  1.62 us

profile of v3, /device:TPU:1, one launch (start us, length us, event | category | flops | bytes accessed | tf_op | source)
XLA Modules:
  0.0 79.7 jit_solution(16397886018909715832)
XLA Ops:
  0.6 77.5 %shard_map.68 = (f32[32,1536]{1,0:T(8,128)}, f32[32,64]{1,0:T(8,128)}) custom-call(bf16[1536,512]{1,0:T(8,128)(2,1)} %act.1, bf16[1536,1792]{1,0:T(8,128)(2,1)} %dl.1, bf16[512,128]{1,0:T(8,128)(2,1)} %qi.1, bf16[1792,128]{1,0:T(8,128)(2,1)} %qo.1, s32[12,128]{1,0:T(8,128)} %bitcast.3), custom_call_target="tpu_custom_call" | custom-call | tf_op jit(solution)/shard_map/pallas_call | solution.py:393
  78.1 1.6 %shard_map.69 = (f32[32,1536]{1,0:T(8,128)}, f32[32,64]{1,0:T(8,128)}) custom-call(f32[32,1536]{1,0:T(8,128)} %get-tuple-element.6.a, f32[32,64]{1,0:T(8,128)} %get-tuple-element.7.b), custom_call_target="tpu_custom_call" | custom-call | tf_op jit(solution)/shard_map/pallas_call | solution.py:432

commit v4 on v3

--- a/solution.py
+++ b/solution.py
@@ -23,7 +23,7 @@
 HA, HB, RMA, RMB, RPA, RPB, XH = range(7)
 KQ = K // 4
 GR = 16
-CR = CH + GR
+CR = CH + 8
 UNIT = 32704.0
 
 
@@ -41,7 +41,7 @@
         top = jnp.ceil(jnp.log2(top))
         codes.append(jnp.round(part * (jnp.exp2(-top) * F32(UNIT))))
         tops.append(top)
-    tops.append(jnp.zeros((GR - CH // GR, x.shape[1]), F32))
+    tops.append(jnp.zeros((8 - CH // GR, x.shape[1]), F32))
     rows = codes + [jnp.concatenate(tops, axis=0)]
     return jnp.concatenate(rows, axis=0).astype(jnp.int32).astype(jnp.int16)
 
@@ -57,8 +57,8 @@
 
 
 def kernel(
-    act, dl, qi, qo, ids, scores_out, docs_out,
-    a_in, a_out, q, p, dbuf, sb, rb, fin, acc, cnt, oh, every, msga, msgb, ga, gb, dpa, dpb,
+    act, dl, qi, qo, ids_in, scores_out, docs_out,
+    a_in, a_out, q, p, dbuf, sb, rb, fin, acc, cnt, oh, every, ids, msga, msgb, ga, gb, dpa, dpb,
     lsem, qs, qr, rs, rr, ms, mr, gs, gr, ds_, dr,
 ):
     dp = lax.axis_index("dp")
@@ -79,37 +79,16 @@
         pltpu.make_async_copy(qo, q.at[0, pl.ds(KIN, KOUT)], lsem.at[1]),
         pltpu.make_async_copy(act, a_in, lsem.at[2]),
         pltpu.make_async_copy(dl, a_out, lsem.at[3]),
+        pltpu.make_async_copy(ids_in, ids, lsem.at[4]),
     ]
     for cp in loads:
         cp.start()
 
     barrier = pltpu.get_barrier_semaphore()
-    for k in range(1, 16):
-        pl.semaphore_signal(
-            barrier, inc=1, device_id={"dp": dp, "tensor": (t + k) % 16}, device_id_type=MESH
-        )
-    for k in range(1, 8):
-        pl.semaphore_signal(
-            barrier, inc=1, device_id={"dp": (dp + k) % 8, "tensor": t}, device_id_type=MESH
-        )
-
-    slot = c * 8 + z * 2 + hx
-    at = slot * CH
-    line, off = at // 128, at % 128
-    one = jnp.broadcast_to(ids[pl.ds(line, 1), :], (8, 128))
-    two = jnp.broadcast_to(ids[pl.ds(jnp.minimum(line + 1, ROWS // 128 - 1), 1), :], (8, 128))
-    lane = lax.broadcasted_iota(jnp.int32, (8, 128), 1)
-    turn = (128 - off) % 128
-    seen = jnp.where(lane < 128 - off, pltpu.roll(one, turn, 1), pltpu.roll(two, turn, 1))
-    seen = jnp.where(lane < CH, seen, -1000)[:1]
-    doc = lax.broadcasted_iota(jnp.int32, (128, 128), 0)
-    oh[...] = (doc == seen).astype(F32)
-    cnt[...] = nt(jnp.ones((8, 128), F32), (doc - 64 == seen).astype(F32))
-    for i in range(ROWS // 128):
-        group = ids[pl.ds(i, 1), :]
-        every[:, pl.ds(i * 128, 128)] = (doc == group).astype(jnp.bfloat16)
-
-    pl.semaphore_wait(barrier, 22)
+    near = (x_lo, y_up, y_dn, x_hi, z_up, z_dn, mate)
+    for to in near:
+        pl.semaphore_signal(barrier, inc=1, device_id=to, device_id_type=MESH)
+    pl.semaphore_wait(barrier, len(near))
 
     sent = []
 
@@ -136,8 +115,8 @@
     q1b = qsend(3, 0, 1, hi, x_lo)
     q3b = qsend(4, 0, 3, hi, y_up)
     q2a = qsend(5, 0, 2, lo, y_dn)
-    loads[2].wait()
-    loads[3].wait()
+
+    slot = c * 8 + z * 2 + hx
 
     moves = {}
 
@@ -177,7 +156,7 @@
             cp.start()
         return cp
 
-    def mm(*bs):
+    def mm(*bs, between=lambda: None):
         def first(i, carry):
             tile(bs, pl.ds(pl.multiple_of(other + i * TM, TM), TM))
             for b in bs:
@@ -189,6 +168,7 @@
             return carry
 
         lax.fori_loop(0, pieces, first, 0)
+        between()
         lax.fori_loop(0, pieces, rest, 0)
         for b in bs:
             for i in range(pieces):
@@ -200,6 +180,8 @@
             moves[b, "core", i].wait_recv()
         code(b, HA, chip(b, 2, 0), z_up)
         code(b, HB, chip(b, 2, 1), z_dn)
+
+    def s1b(b):
         code(b, RMB, chip(b, 1, 1), z_up)
         code(b, RPA, chip(b, 3, 0), z_dn)
 
@@ -316,8 +298,26 @@
         q5[n].wait_recv()
         q7.append(qsend(14 + n, 5, 7, quarter[n], y_dn))
 
+    loads[2].wait()
+    loads[3].wait()
     mm(0)
     s1(0)
+    s1b(0)
+    loads[4].wait()
+    at = slot * CH
+    line, off = at // 128, at % 128
+    one = jnp.broadcast_to(ids[pl.ds(line, 1), :], (8, 128))
+    two = jnp.broadcast_to(ids[pl.ds(jnp.minimum(line + 1, ROWS // 128 - 1), 1), :], (8, 128))
+    lane = lax.broadcasted_iota(jnp.int32, (8, 128), 1)
+    turn = (128 - off) % 128
+    seen = jnp.where(lane < 128 - off, pltpu.roll(one, turn, 1), pltpu.roll(two, turn, 1))
+    seen = jnp.where(lane < CH, seen, -1000)[:1]
+    doc = lax.broadcasted_iota(jnp.int32, (128, 128), 0)
+    oh[...] = (doc == seen).astype(F32)
+    cnt[...] = nt(jnp.ones((8, 128), F32), (doc - 64 == seen).astype(F32))
+    for i in range(ROWS // 128):
+        group = ids[pl.ds(i, 1), :]
+        every[:, pl.ds(i * 128, 128)] = (doc == group).astype(jnp.bfloat16)
     s2(0)
     q3a.wait_recv()
     q4a = qsend(6, 3, 4, lo, y_up)
@@ -332,46 +332,49 @@
     q5 += [qsend(12, 2, 5, quarter[2], x_lo), qsend(13, 2, 5, quarter[3], x_lo)]
     q1b.wait_recv()
     q6b = qsend(9, 1, 6, hi, y_up)
-    mm(1, 2)
-    forward(0)
+    mm(1)
+    q3b.wait_recv()
     s1(1)
+    s1b(1)
+    mm(2, 3, between=lambda: forward(0))
+    forward(1)
     s1(2)
-    q3b.wait_recv()
-    mm(3)
-    forward(1)
+    s1b(2)
     s2(1)
     s1(3)
+    s1b(3)
     forward(2)
     q4a.wait_recv()
     q4b.wait_recv()
-    mm(4)
-    s2(2)
+    mm(4, between=lambda: s2(2))
     forward(3)
     s1(4)
+    s1b(4)
     s3(1)
     s2(3)
-    mm(5)
-    s3(2)
+    mm(5, between=lambda: s3(2))
     s1(5)
+    s1b(5)
+    s2(4)
     s4(0)
-    s2(4)
     s3(3)
     for cp in (q6a, q6b, *q7):
         cp.wait_recv()
-    mm(6, 7)
+    mm(6, 7, between=lambda: s2(5))
+    s1(6)
+    s1(7)
+    s1b(6)
+    s1b(7)
     s4(1)
     s4(2)
-    s2(5)
     s3(4)
-    s1(6)
-    s1(7)
     s4(3)
+    s2(6)
+    s2(7)
     s3(5)
-    s2(6)
     s4(4)
-    s2(7)
+    s3(6)
     s4(5)
-    s3(6)
     s3(7)
     shared_a = share_a()
     s4(6)
@@ -396,7 +399,7 @@
             jax.ShapeDtypeStruct((32, ROWS), F32),
             jax.ShapeDtypeStruct((32, 64), F32),
         ),
-        in_specs=[any_, any_, any_, any_, vmem],
+        in_specs=[any_] * 5,
         out_specs=(vmem, vmem),
         scratch_shapes=[
             pltpu.VMEM((ROWS, KIN), jnp.bfloat16),
@@ -411,13 +414,14 @@
             pltpu.VMEM((8, 128), F32),
             pltpu.VMEM((128, 128), F32),
             pltpu.VMEM((128, ROWS), jnp.bfloat16),
+            pltpu.VMEM((ROWS // 128, 128), jnp.int32),
             pltpu.VMEM((24, 128), F32),
             pltpu.VMEM((16, 128), F32),
             pltpu.VMEM((16, 24, 128), F32),
             pltpu.VMEM((16, 16, 128), F32),
             pltpu.VMEM((8, 32, 128), F32),
             pltpu.VMEM((8, 8, 128), F32),
-            dma((4,)), dma((18,)), dma((18,)), dma((7, NB)), dma((7, NB)),
+            dma((5,)), dma((18,)), dma((18,)), dma((7, NB)), dma((7, NB)),
             dma((NB, HALF // TM)), dma((NB, HALF // TM)),
             dma((2, 15)), dma((2, 15)), dma((2, 7)), dma((2, 7)),
         ],

time: 79.9 us -> 74.8 us (0.936)
  Pallas kernels: 79.1 us -> 74 us
    pallas_call x1, Pallas kernels: 77.5 us -> 72.4 us  [body(): pl.pallas_call(kernel, out_shape=(jax.ShapeDtypeStruct((32, ROWS), F32),...]
where the time goes in v4:
time: 74.8 us; the launch traced here: 74.7 us
  Pallas kernels  74 us (99%)
    pallas_call x1, Pallas kernels, body(): pl.pallas_call(kernel, out_shape=(jax.ShapeDtypeStruct((32, ROWS), F32),...  72.4 us
    pallas_call x1, Pallas kernels, body(): pl.pallas_call(finish, out_shape=(jax.ShapeDtypeStruct((32, ROWS), F32),...  1.62 us

profile of v4, /device:TPU:1, one launch (start us, length us, event | category | flops | bytes accessed | tf_op | source)
XLA Modules:
  0.0 74.7 jit_solution(9689983940361552841)
XLA Ops:
  0.6 72.4 %shard_map.68 = (f32[32,1536]{1,0:T(8,128)}, f32[32,64]{1,0:T(8,128)}) custom-call(bf16[1536,512]{1,0:T(8,128)(2,1)} %act.1, bf16[1536,1792]{1,0:T(8,128)(2,1)} %dl.1, bf16[512,128]{1,0:T(8,128)(2,1)} %qi.1, bf16[1792,128]{1,0:T(8,128)(2,1)} %qo.1, s32[12,128]{1,0:T(8,128)} %bitcast.3), custom_call_target="tpu_custom_call" | custom-call | tf_op jit(solution)/shard_map/pallas_call | solution.py:396
  73.1 1.6 %shard_map.69 = (f32[32,1536]{1,0:T(8,128)}, f32[32,64]{1,0:T(8,128)}) custom-call(f32[32,1536]{1,0:T(8,128)} %get-tuple-element.6.a, f32[32,64]{1,0:T(8,128)} %get-tuple-element.7.b), custom_call_target="tpu_custom_call" | custom-call | tf_op jit(solution)/shard_map/pallas_call | solution.py:436

commit v5 on v4

--- a/solution.py
+++ b/solution.py
@@ -57,9 +57,9 @@
 
 
 def kernel(
-    act, dl, qi, qo, ids_in, scores_out, docs_out,
-    a_in, a_out, q, p, dbuf, sb, rb, fin, acc, cnt, oh, every, ids, msga, msgb, ga, gb, dpa, dpb,
-    lsem, qs, qr, rs, rr, ms, mr, gs, gr, ds_, dr,
+    act, dl, qi, qo, ids_in, scores_hbm, docs_out,
+    a_in, a_out, q, p, dbuf, sb, rb, fin, acc, cnt, oh, every, ids, scores_out, msga, msgb, ga, gb, dpa, dpb,
+    lsem, ss, qr, rr, mr, gr, dr,
 ):
     dp = lax.axis_index("dp")
     t = lax.axis_index("tensor")
@@ -90,22 +90,19 @@
         pl.semaphore_signal(barrier, inc=1, device_id=to, device_id_type=MESH)
     pl.semaphore_wait(barrier, len(near))
 
-    sent = []
-
-    def send(src, dst, ss, rsem, to):
+    def send(src, dst, ssem, rsem, to):
         cp = pltpu.make_async_remote_copy(
-            src_ref=src, dst_ref=dst, send_sem=ss, recv_sem=rsem,
+            src_ref=src, dst_ref=dst, send_sem=ssem, recv_sem=rsem,
             device_id=to, device_id_type=MESH,
         )
         cp.start()
-        sent.append(cp)
         return cp
 
     lo, hi = pl.ds(0, KH), pl.ds(KH, KH)
     quarter = [pl.ds(i * KQ, KQ) for i in (2, 3, 0, 1)]
 
     def qsend(n, src, dst, rows, to):
-        return send(q.at[src, rows], q.at[dst, rows], qs.at[n], qr.at[n], to)
+        return send(q.at[src, rows], q.at[dst, rows], ss.at[0], qr.at[n], to)
 
     loads[0].wait()
     loads[1].wait()
@@ -121,7 +118,7 @@
     moves = {}
 
     def rsend(b, role, src, dst, to):
-        moves[b, role] = send(src, dst, rs.at[role, b], rr.at[role, b], to)
+        moves[b, role] = send(src, dst, ss.at[1], rr.at[role, b], to)
 
     own, other = c * HALF, (1 - c) * HALF
 
@@ -149,7 +146,7 @@
         cp = pltpu.make_async_remote_copy(
             src_ref=p.at[b, rows],
             dst_ref=dbuf.at[b, pl.ds(pl.multiple_of(i * TM, TM), TM)],
-            send_sem=ms.at[b, i], recv_sem=mr.at[b, i],
+            send_sem=ss.at[2], recv_sem=mr.at[b, i],
             device_id=mate, device_id_type=MESH,
         )
         if start:
@@ -173,7 +170,6 @@
         for b in bs:
             for i in range(pieces):
                 moves[b, "core", i] = piece(b, i)
-                sent.append(moves[b, "core", i])
 
     def s1(b):
         for i in range(pieces):
@@ -214,13 +210,18 @@
         pick = jnp.where(row == (b % 2) * 4 + col // RANK, F32(RANK ** -0.5), F32(0))
         acc[b] = nt(pick, prod)
 
+    def every_one(buf, n, ssem, rsem):
+        return pltpu.make_async_remote_copy(
+            src_ref=buf.at[pl.ds(0, n)], dst_ref=buf.at[pl.ds(0, n)], send_sem=ssem,
+            recv_sem=rsem, device_id=mate, device_id_type=MESH,
+        )
+
     def spread(msg, g, n):
         g[slot] = msg[...]
-        got = []
         for k in range(1, 16):
             to = {"dp": dp, "tensor": (t + k) % 16}
-            got.append(send(msg, g.at[slot], gs.at[n, k - 1], gr.at[n, k - 1], to))
-        return got
+            send(msg, g.at[slot], ss.at[3 + n], gr.at[n], to)
+        return every_one(g, 15, ss.at[3 + n], gr.at[n])
 
     def share_a():
         for b in range(0, 6, 2):
@@ -246,8 +247,7 @@
         return jnp.concatenate([g[m, pl.ds(0, rows), :][:, :CH] for m in range(16)], axis=1)
 
     def finish_a(got):
-        for cp in got:
-            cp.wait_recv()
+        got.wait_recv()
         found = gathered(ga, 24)
         scores_out[...] = rows_of(0, 6, found, jnp.zeros((32, ROWS), F32))
         one = found.astype(jnp.bfloat16)
@@ -262,8 +262,7 @@
         return across(dpa, rows_of(0, 6, sums, jnp.zeros((32, 128), F32)), 0)
 
     def finish_b(got):
-        for cp in got:
-            cp.wait_recv()
+        got.wait_recv()
         part = gb[0, pl.ds(8, 8), :]
         for m in range(1, 16):
             part = part + gb[m, pl.ds(8, 8), :]
@@ -271,20 +270,17 @@
 
     def across(buf, part, n):
         buf[dp] = part
-        got = []
         for k in range(1, 8):
             to = {"dp": (dp + k) % 8, "tensor": t}
-            got.append(send(buf.at[dp], buf.at[dp], ds_.at[n, k - 1], dr.at[n, k - 1], to))
-        return got
+            send(buf.at[dp], buf.at[dp], ss.at[5 + n], dr.at[n], to)
+        return every_one(buf, 7, ss.at[5 + n], dr.at[n])
 
     def mean(early, late):
-        for cp in early:
-            cp.wait_recv()
+        early.wait_recv()
         whole = dpa[0]
         for m in range(1, 8):
             whole = whole + dpa[m]
-        for cp in late:
-            cp.wait_recv()
+        late.wait_recv()
         for m in range(8):
             where = [(1 - m // 4) * 4 + (m + 3) % 4, (1 - m // 4) * 4 + (m + 2) % 4]
             whole = whole + rows_of(0, 2, dpb[m], jnp.zeros((32, 128), F32), where)
@@ -346,18 +342,18 @@
     forward(2)
     q4a.wait_recv()
     q4b.wait_recv()
-    mm(4, between=lambda: s2(2))
+    mm(4)
+    s2(2)
     forward(3)
     s1(4)
     s1b(4)
     s3(1)
     s2(3)
-    mm(5, between=lambda: s3(2))
+    mm(5)
     s1(5)
     s1b(5)
+    s3(2)
     s2(4)
-    s4(0)
-    s3(3)
     for cp in (q6a, q6b, *q7):
         cp.wait_recv()
     mm(6, 7, between=lambda: s2(5))
@@ -365,6 +361,8 @@
     s1(7)
     s1b(6)
     s1b(7)
+    s3(3)
+    s4(0)
     s4(1)
     s4(2)
     s3(4)
@@ -383,9 +381,17 @@
     early = finish_a(shared_a)
     late = finish_b(shared_b)
     scores_out[...] = rows_of(6, 8, gathered(gb, 8), scores_out[...])
+    out = pltpu.make_async_copy(scores_out, scores_hbm, lsem.at[0])
+    out.start()
     mean(early, late)
-    for cp in sent:
-        cp.wait_send()
+    every_one(q, 7, ss.at[0], ss.at[0]).wait_send()
+    every_one(sb, NB, ss.at[1], ss.at[1]).wait_send()
+    every_one(dbuf, NB, ss.at[2], ss.at[2]).wait_send()
+    shared_a.wait_send()
+    shared_b.wait_send()
+    early.wait_send()
+    late.wait_send()
+    out.wait()
 
 
 def body(activations, deltas, query_in, query_out, doc_ids):
@@ -400,7 +406,7 @@
             jax.ShapeDtypeStruct((32, 64), F32),
         ),
         in_specs=[any_] * 5,
-        out_specs=(vmem, vmem),
+        out_specs=(any_, vmem),
         scratch_shapes=[
             pltpu.VMEM((ROWS, KIN), jnp.bfloat16),
             pltpu.VMEM((ROWS, KOUT), jnp.bfloat16),
@@ -415,15 +421,14 @@
             pltpu.VMEM((128, 128), F32),
             pltpu.VMEM((128, ROWS), jnp.bfloat16),
             pltpu.VMEM((ROWS // 128, 128), jnp.int32),
+            pltpu.VMEM((32, ROWS), F32),
             pltpu.VMEM((24, 128), F32),
             pltpu.VMEM((16, 128), F32),
             pltpu.VMEM((16, 24, 128), F32),
             pltpu.VMEM((16, 16, 128), F32),
             pltpu.VMEM((8, 32, 128), F32),
             pltpu.VMEM((8, 8, 128), F32),
-            dma((5,)), dma((18,)), dma((18,)), dma((7, NB)), dma((7, NB)),
-            dma((NB, HALF // TM)), dma((NB, HALF // TM)),
-            dma((2, 15)), dma((2, 15)), dma((2, 7)), dma((2, 7)),
+            dma((5,)), dma((7,)), dma((18,)), dma((7, NB)), dma((NB, HALF // TM)), dma((2,)), dma((2,)),
         ],
         compiler_params=pltpu.CompilerParams(
             collective_id=0, has_side_effects=True, vmem_limit_bytes=60 * 1024 * 1024

time: 74.8 us -> 73 us (0.976)
  Pallas kernels: 74 us -> 72.2 us
    pallas_call x1, Pallas kernels: 72.4 us -> 70.6 us  [body(): pl.pallas_call(kernel, out_shape=(jax.ShapeDtypeStruct((32, ROWS), F32),...]
where the time goes in v5:
time: 73 us; the launch traced here: 72.8 us
  Pallas kernels  72.2 us (99%)
    pallas_call x1, Pallas kernels, body(): pl.pallas_call(kernel, out_shape=(jax.ShapeDtypeStruct((32, ROWS), F32),...  70.6 us
    pallas_call x1, Pallas kernels, body(): pl.pallas_call(finish, out_shape=(jax.ShapeDtypeStruct((32, ROWS), F32),...  1.62 us

profile of v5, /device:TPU:1, one launch (start us, length us, event | category | flops | bytes accessed | tf_op | source)
XLA Modules:
  0.0 72.8 jit_solution(5599170506521355747)
XLA Ops:
  0.6 70.6 %shard_map.68 = (f32[32,1536]{1,0:T(8,128)}, f32[32,64]{1,0:T(8,128)}) custom-call(bf16[1536,512]{1,0:T(8,128)(2,1)} %act.1, bf16[1536,1792]{1,0:T(8,128)(2,1)} %dl.1, bf16[512,128]{1,0:T(8,128)(2,1)} %qi.1, bf16[1792,128]{1,0:T(8,128)(2,1)} %qo.1, s32[12,128]{1,0:T(8,128)} %bitcast.3), custom_call_target="tpu_custom_call" | custom-call | tf_op jit(solution)/shard_map/pallas_call | solution.py:402
  71.2 1.6 %shard_map.69 = (f32[32,1536]{1,0:T(8,128)}, f32[32,64]{1,0:T(8,128)}) custom-call(f32[32,1536]{1,0:T(8,128)} %get-tuple-element.6.a, f32[32,64]{1,0:T(8,128)} %get-tuple-element.7.b), custom_call_target="tpu_custom_call" | custom-call | tf_op jit(solution)/shard_map/pallas_call | solution.py:441

commit v6 on v5

--- a/solution.py
+++ b/solution.py
@@ -19,7 +19,7 @@
 K = KIN + KOUT
 KH = K // 2
 NB = 8
-TM = 256
+TM = HALF // 2
 HA, HB, RMA, RMB, RPA, RPB, XH = range(7)
 KQ = K // 4
 GR = 16
@@ -141,43 +141,46 @@
 
     pieces = HALF // TM
 
-    def piece(b, i, start=False):
-        rows = pl.ds(pl.multiple_of(other + i * TM, TM), TM)
+    def sect(k, base):
+        return pl.ds(pl.multiple_of(base + ((z + 2) % 4 // 2 + k) % 2 * TM, TM), TM)
+
+    def piece(b, k, start=False):
         cp = pltpu.make_async_remote_copy(
-            src_ref=p.at[b, rows],
-            dst_ref=dbuf.at[b, pl.ds(pl.multiple_of(i * TM, TM), TM)],
-            send_sem=ss.at[2], recv_sem=mr.at[b, i],
-            device_id=mate, device_id_type=MESH,
+            src_ref=p.at[b, sect(k, other)], dst_ref=dbuf.at[b, sect(k, 0)],
+            send_sem=ss.at[2], recv_sem=mr.at[b, k], device_id=mate, device_id_type=MESH,
         )
         if start:
             cp.start()
         return cp
 
     def mm(*bs, between=lambda: None):
-        def first(i, carry):
-            tile(bs, pl.ds(pl.multiple_of(other + i * TM, TM), TM))
-            for b in bs:
-                piece(b, i, True)
-            return carry
-
-        def rest(i, carry):
-            tile(bs, pl.ds(pl.multiple_of(own + i * TM, TM), TM))
-            return carry
-
-        lax.fori_loop(0, pieces, first, 0)
+        def part(k):
+            def step(i, carry):
+                tile(bs, sect(k, (1 - c + i) % 2 * HALF))
+
+                @pl.when(i == 0)
+                def _():
+                    for b in bs:
+                        piece(b, k, True)
+
+                return carry
+
+            lax.fori_loop(0, 2, step, 0)
+
+        part(0)
         between()
-        lax.fori_loop(0, pieces, rest, 0)
-        for b in bs:
-            for i in range(pieces):
-                moves[b, "core", i] = piece(b, i)
+        part(1)
+
+    def met(b, k):
+        piece(b, k).wait_recv()
 
     def s1(b):
-        for i in range(pieces):
-            moves[b, "core", i].wait_recv()
+        met(b, 0)
         code(b, HA, chip(b, 2, 0), z_up)
         code(b, HB, chip(b, 2, 1), z_dn)
 
     def s1b(b):
+        met(b, 1)
         code(b, RMB, chip(b, 1, 1), z_up)
         code(b, RPA, chip(b, 3, 0), z_dn)
 
@@ -328,9 +331,8 @@
     q5 += [qsend(12, 2, 5, quarter[2], x_lo), qsend(13, 2, 5, quarter[3], x_lo)]
     q1b.wait_recv()
     q6b = qsend(9, 1, 6, hi, y_up)
-    mm(1)
+    mm(1, between=lambda: s1(1))
     q3b.wait_recv()
-    s1(1)
     s1b(1)
     mm(2, 3, between=lambda: forward(0))
     forward(1)
@@ -349,16 +351,19 @@
     s1b(4)
     s3(1)
     s2(3)
-    mm(5)
-    s1(5)
+    mm(5, between=lambda: s1(5))
     s1b(5)
     s3(2)
     s2(4)
     for cp in (q6a, q6b, *q7):
         cp.wait_recv()
-    mm(6, 7, between=lambda: s2(5))
-    s1(6)
-    s1(7)
+
+    def ends():
+        s2(5)
+        s1(6)
+        s1(7)
+
+    mm(6, 7, between=ends)
     s1b(6)
     s1b(7)
     s3(3)
@@ -366,10 +371,10 @@
     s4(1)
     s4(2)
     s3(4)
-    s4(3)
     s2(6)
     s2(7)
     s3(5)
+    s4(3)
     s4(4)
     s3(6)
     s4(5)

time: 73 us -> 71.9 us (0.985)
  Pallas kernels: 72.2 us -> 71.2 us
    pallas_call x1, Pallas kernels: 70.6 us -> 69.5 us  [body(): pl.pallas_call(kernel, out_shape=(jax.ShapeDtypeStruct((32, ROWS), F32),...]
where the time goes in v6:
time: 71.9 us; the launch traced here: 71.8 us
  Pallas kernels  71.2 us (99%)
    pallas_call x1, Pallas kernels, body(): pl.pallas_call(kernel, out_shape=(jax.ShapeDtypeStruct((32, ROWS), F32),...  69.5 us
    pallas_call x1, Pallas kernels, body(): pl.pallas_call(finish, out_shape=(jax.ShapeDtypeStruct((32, ROWS), F32),...  1.62 us

profile of v6, /device:TPU:1, one launch (start us, length us, event | category | flops | bytes accessed | tf_op | source)
XLA Modules:
  0.0 71.8 jit_solution(6062503770474293046)
XLA Ops:
  0.6 69.5 %shard_map.68 = (f32[32,1536]{1,0:T(8,128)}, f32[32,64]{1,0:T(8,128)}) custom-call(bf16[1536,512]{1,0:T(8,128)(2,1)} %act.1, bf16[1536,1792]{1,0:T(8,128)(2,1)} %dl.1, bf16[512,128]{1,0:T(8,128)(2,1)} %qi.1, bf16[1792,128]{1,0:T(8,128)(2,1)} %qo.1, s32[12,128]{1,0:T(8,128)} %bitcast.3), custom_call_target="tpu_custom_call" | custom-call | tf_op jit(solution)/shard_map/pallas_call | solution.py:407
  70.2 1.6 %shard_map.69 = (f32[32,1536]{1,0:T(8,128)}, f32[32,64]{1,0:T(8,128)}) custom-call(f32[32,1536]{1,0:T(8,128)} %get-tuple-element.6.a, f32[32,64]{1,0:T(8,128)} %get-tuple-element.7.b), custom_call_target="tpu_custom_call" | custom-call | tf_op jit(solution)/shard_map/pallas_call | solution.py:446

commit v7 on v6

--- a/solution.py
+++ b/solution.py
@@ -377,8 +377,8 @@
     s4(3)
     s4(4)
     s3(6)
+    s3(7)
     s4(5)
-    s3(7)
     shared_a = share_a()
     s4(6)
     s4(7)

time: 71.9 us -> 71.9 us (level)
  no operation moved by 1% of the time
where the time goes in v7:
time: 71.9 us; the launch traced here: 71.8 us
  Pallas kernels  71.1 us (99%)
    pallas_call x1, Pallas kernels, body(): pl.pallas_call(kernel, out_shape=(jax.ShapeDtypeStruct((32, ROWS), F32),...  69.5 us
    pallas_call x1, Pallas kernels, body(): pl.pallas_call(finish, out_shape=(jax.ShapeDtypeStruct((32, ROWS), F32),...  1.62 us

profile of v7, /device:TPU:1, one launch (start us, length us, event | category | flops | bytes accessed | tf_op | source)
XLA Modules:
  0.0 71.8 jit_solution(10052827828036049503)
XLA Ops:
  0.6 69.5 %shard_map.68 = (f32[32,1536]{1,0:T(8,128)}, f32[32,64]{1,0:T(8,128)}) custom-call(bf16[1536,512]{1,0:T(8,128)(2,1)} %act.1, bf16[1536,1792]{1,0:T(8,128)(2,1)} %dl.1, bf16[512,128]{1,0:T(8,128)(2,1)} %qi.1, bf16[1792,128]{1,0:T(8,128)(2,1)} %qo.1, s32[12,128]{1,0:T(8,128)} %bitcast.3), custom_call_target="tpu_custom_call" | custom-call | tf_op jit(solution)/shard_map/pallas_call | solution.py:407
  70.2 1.6 %shard_map.69 = (f32[32,1536]{1,0:T(8,128)}, f32[32,64]{1,0:T(8,128)}) custom-call(f32[32,1536]{1,0:T(8,128)} %get-tuple-element.6.a, f32[32,64]{1,0:T(8,128)} %get-tuple-element.7.b), custom_call_target="tpu_custom_call" | custom-call | tf_op jit(solution)/shard_map/pallas_call | solution.py:446
